TPU v7x, 32 devices: a whole 2x2x4 slice. The times are simulated.
32 devices in a mesh: col: 16 (over z, y, x), row: 2 (over core).
Axes of the slice: x: 2, y: 2, z: 4, core: 2. Of those that a mesh axis runs over, the one named last changes fastest.
Arguments:
- gradient: bfloat16 [4096, 16384], P('row', 'col'), may hold values from -120 to 120
- momentum: float32 [4096, 16384], P('row', 'col'), may hold values from -6 to 6
- right_factor: float32 [16384, 256], P(('col', 'row')), may hold values from -0.046875 to 0.046875
Outputs:
- momentum_next: float32 [4096, 16384], P('row', 'col')
- right_next: float32 [16384, 256], P(('col', 'row'))
- update: bfloat16 [4096, 16384], P('row', 'col')
All inputs are finite; a program needn't handle non-finite values.
Results may differ from a plain program's by a relative error of at most 0.0012.
Values sent between devices are 32-bit elements; how exact they have to be, the bound alone decides.
No kernel may reach another device: no remote copies, remote signals or barrier semaphores. Data moves between devices by JAX's collectives and lax.ppermute only.
A program may use at most 64 MiB of HBM per device.

v0:
```python
import math
import jax
import jax.numpy as jnp
from jax import lax
from jax.sharding import PartitionSpec as P

M = 4096
N = 16384
RANK = 256
EPS = 1e-06
FEEDBACK = 0.05


def body(gradient, momentum, right_factor):
    highest = lax.Precision.HIGHEST
    blend = momentum + gradient.astype(jnp.float32)
    right_block = lax.all_gather(right_factor, "row", axis=0, tiled=True)
    contract_rows = (((0,), (0,)), ((), ()))
    partial_value = jnp.dot(
        blend, right_block, precision=highest, preferred_element_type=jnp.float32
    )
    left = lax.psum(partial_value, "col")
    local_gram = lax.dot_general(
        left, left, contract_rows, precision=highest, preferred_element_type=jnp.float32
    )
    gram = lax.psum(local_gram, "row")
    lower = jnp.linalg.cholesky(gram)
    left_orth = jax.scipy.linalg.solve_triangular(lower, left.T, lower=True).T
    right_local = lax.dot_general(
        blend, left_orth, contract_rows, precision=highest, preferred_element_type=jnp.float32
    )
    share = lax.psum_scatter(right_local, "row", scatter_dimension=0, tiled=True)
    squares_right = lax.psum(jnp.sum(share * share, axis=0), ("col", "row"))
    right_norm = jnp.sqrt(squares_right + EPS)
    right_next = share / right_norm[None, :]
    right_whole = lax.all_gather(share, "row", axis=0, tiled=True)
    right_unit = right_whole / right_norm[None, :]
    contract_cols = (((1,), (1,)), ((), ()))
    feedback_term = lax.dot_general(
        left_orth, right_whole, contract_cols, precision=highest, preferred_element_type=jnp.float32
    )
    momentum_next = blend - FEEDBACK * feedback_term
    factor = math.sqrt(M * N / RANK)
    direction = lax.dot_general(
        left_orth, right_unit, contract_cols, precision=highest, preferred_element_type=jnp.float32
    )
    update = (factor * direction).astype(jnp.bfloat16)
    return (momentum_next, right_next, update)


def solution(mesh):
    placed = (P("row", "col"), P("row", "col"), P(("col", "row"), None))
    return jax.shard_map(
        body,
        mesh=mesh,
        in_specs=placed,
        out_specs=(P("row", "col"), P(("col", "row"), None), P("row", "col")),
        check_vma=False,
    )
```

profile of v0, /device:TPU:0, one launch (start us, length us, event | category | flops | bytes accessed | tf_op | source)
XLA Modules:
  0.0 361.9 jit_solution(6752334707807662119)
XLA Ops:
  7.2 0.0 all-gather.3.cloned.1.call-start
  7.2 0.7 all-gather.3.cloned.1.call-update
  7.9 0.0 all-reduce.4.cloned.1.call-start
  7.9 13.4 %all-gather.3.cloned.1.call-done = f32[1024,256]{1,0:T(8,128)} async-done(((f32[512,256]{1,0:T(8,128)}), f32[1024,256]{1,0:T(8,128)}) %all-gather.3.cloned.1.call-update) | async-done | bytes 1048592 | tf_op jit(solution)/shard_map/all_gather | solution.py:17
  21.3 11.0 %fusion.1 = f32[2048,256]{1,0:T(8,128)} fusion(f32[1024,256]{1,0:T(8,128)} %all-gather.3.cloned.1.call-done, f32[2048,1024]{1,0:T(8,128)} %param.4, bf16[2048,1024]{1,0:T(8,128)(2,1)} %param.3), kind=kOutput, calls=%fused_computation.6 | convolution fusion | flops 6446645248 | bytes 15728640 | tf_op jit(solution)/shard_map/dot_general | solution.py:19
  32.3 0.0 all-reduce.4.cloned.1.call-update
  32.3 0.0 all-reduce.6.cloned.1.call-start
  32.3 127.9 %all-reduce.4.cloned.1.call-done = f32[2048,256]{1,0:T(8,128)} async-done(((f32[2048,256]{1,0:T(8,128)}), f32[2048,256]{1,0:T(8,128)}) %all-reduce.4.cloned.1.call-update) | async-done | bytes 2097168 | tf_op jit(solution)/shard_map/psum | solution.py:22
  160.2 0.0 copy-start.2
  160.2 6.5 %fusion.16 = f32[256,256]{0,1:T(8,128)} fusion(f32[2048,256]{1,0:T(8,128)} %all-reduce.4.cloned.1.call-done), kind=kOutput, calls=%fused_computation.42 | convolution fusion | flops 1610612736 | bytes 2359296 | tf_op jit(solution)/shard_map/dot_general | solution.py:23
  166.7 0.0 all-reduce.6.cloned.1.call-update
  166.8 0.6 reduce-scatter.2.cloned.1.call-start
  167.3 17.0 %all-reduce.6.cloned.1.call-done = f32[256,256]{0,1:T(8,128)} async-done(((f32[256,256]{0,1:T(8,128)}), f32[256,256]{0,1:T(8,128)}) %all-reduce.6.cloned.1.call-update) | async-done | bytes 262160 | tf_op jit(solution)/shard_map/psum | solution.py:26
  184.4 1.1 copy.7
  185.5 1.0 fusion.6
  186.5 11.7 %cholesky.50 = f32[128,128]{1,0:T(8,128)S(1)} custom-call(f32[128,128]{1,0:T(8,128)S(1)} %cholesky.118), custom_call_target="Cholesky" | custom-call | tf_op jit(solution)/shard_map/jit(cholesky)/cholesky | solution.py:27
  198.2 9.8 %custom-call.15 = f32[1,128,128]{1,2,0:T(8,128)S(1)} custom-call(f32[1,128,128]{2,1,0:T(8,128)S(1)} %get-tuple-element.24), custom_call_target="InvertDiagBlocksLowerTriangular" | custom-call | tf_op jit(solution)/shard_map/jit(cholesky)/cholesky | solution.py:27
  208.1 0.2 constant_dynamic-update-slice_fusion.1
  208.3 0.3 convolution_subtract_fusion.1
  208.5 11.7 %cholesky.105 = f32[128,128]{1,0:T(8,128)S(1)} custom-call(f32[128,128]{1,0:T(8,128)S(1)} %convolution_subtract_fusion.1), custom_call_target="Cholesky" | custom-call | tf_op jit(solution)/shard_map/jit(cholesky)/cholesky | solution.py:27
  220.3 0.6 compare_reduce_fusion
  222.3 0.1 triangular_solve.57
  222.3 4.2 %while.1 = (s32[]{:T(128)}, f32[256,256]{1,0:T(8,128)S(1)}, s32[2,2]{1,0:T(2,128)S(1)}, f32[2,128,128]{2,1,0:T(8,128)S(1)}, s32[]{:T(128)}) while((s32[]{:T(128)}, f32[256,256]{1,0:T(8,128)S(1)}, s32[2,2]{1,0:T(2,128)S(1)}, f32[2,128,128]{2,1,0:T(8,128)S(1)}, s32[]{:T(128)}) %tuple.27), condition=%wide.while_cond, body=%wide.while_body.sunk | while | flops 2 | bytes 131189 | solution.py:28
  222.5 0.6 fusion.26
  223.1 1.4 bitcast_dynamic-update-slice_fusion.2
  224.5 0.6 fusion.26
  225.1 1.4 bitcast_dynamic-update-slice_fusion.2
  226.5 19.7 %custom-call.16 = f32[2,128,128]{1,2,0:T(8,128)S(1)} custom-call(f32[2,128,128]{2,1,0:T(8,128)S(1)} %get-tuple-element.10), custom_call_target="InvertDiagBlocksLowerTriangular" | custom-call | tf_op jit(solution)/shard_map/jit(_solve_triangular)/triangular_solve | solution.py:28
  246.2 0.0 copy-start
  246.2 0.0 copy-done.2
  246.2 1.1 fusion.2
  247.3 1.8 convolution_subtract_fusion
  249.1 1.1 fusion.8
  250.2 0.0 copy-done
  250.2 16.6 %fusion = f32[1024,256]{1,0:T(8,128)} fusion(f32[2048,1024]{1,0:T(8,128)} %param.4, bf16[2048,1024]{1,0:T(8,128)(2,1)S(1)} %copy-done, f32[128,2048]{1,0:T(8,128)S(1)} %fusion.8, f32[128,2048]{1,0:T(8,128)S(1)} %fusion.2), kind=kOutput, calls=%fused_computation.5 | convolution fusion | flops 6447169536 | bytes 15728640 | tf_op jit(solution)/shard_map/dot_general | solution.py:29
  266.8 0.0 reduce-scatter.2.cloned.1.call-update
  266.9 0.0 all-gather.5.cloned.1.call-start
  266.9 9.7 %reduce-scatter.2.cloned.1.call-done = f32[512,256]{1,0:T(8,128)} async-done(((f32[1024,256]{1,0:T(8,128)}), f32[512,256]{1,0:T(8,128)}) %reduce-scatter.2.cloned.1.call-update) | async-done | bytes 524304 | tf_op jit(solution)/shard_map/reduce_scatter | solution.py:32
  276.6 0.0 all-gather.5.cloned.1.call-update
  276.6 1.1 multiply_reduce_fusion
  277.8 40.8 %psum.23 = f32[256]{0:T(256)S(1)} all-reduce(f32[256]{0:T(256)S(1)} %multiply_reduce_fusion), channel_id=1, replica_groups=mesh['col'=16,'row'=2] {'col','row'}, use_global_device_ids=true, to_apply=%region_8.9 | all-reduce | flops 256 | bytes 2048 | tf_op jit(solution)/shard_map/psum | solution.py:33
  318.6 1.9 broadcast_divide_fusion
  320.5 0.0 all-gather.5.cloned.1.call-done
  320.5 0.0 copy-start.1
  320.5 0.0 copy-start.3
  320.5 16.1 %multiply_convert_fusion = bf16[2048,1024]{1,0:T(8,128)(2,1)} fusion(f32[128,2048]{1,0:T(8,128)S(1)} %fusion.8, f32[128,2048]{1,0:T(8,128)S(1)} %fusion.2, f32[1024,256]{1,0:T(8,128)} %all-gather.5.cloned.1.call-done, f32[256]{0:T(256)S(1)} %add_sqrt_fusion), kind=kOutput, calls=%fused_computation.2 | convolution fusion | flops 6447431680 | bytes 7341056 | tf_op jit(solution)/shard_map/dot_general | solution.py:44
  336.6 0.0 copy-done.1
  336.6 0.0 copy-done.3
  336.6 18.4 %multiply_subtract_fusion = f32[2048,1024]{1,0:T(8,128)} fusion(f32[1024,256]{1,0:T(8,128)S(1)} %copy-done.3, f32[2048,1024]{1,0:T(8,128)} %param.4, bf16[2048,1024]{1,0:T(8,128)(2,1)S(1)} %copy-done.1, f32[128,2048]{1,0:T(8,128)S(1)} %fusion.8, f32[128,2048]{1,0:T(8,128)S(1)} %fusion.2), kind=kOutput, calls=%fused_computation.3 | convolution fusion | flops 6451363840 | bytes 24117248 | tf_op jit(solution)/shard_map/dot_general | solution.py:39
  (10 shorter events, 0.2 us)
Async XLA Ops:
  7.2 14.1 %all-gather.3.cloned.1.call-start = ((), (), s32[]{:S(2)}) async-start(), calls=%async_computation.1 | async-start | bytes 1572864 | tf_op jit(solution)/shard_map/all_gather | solution.py:17
  7.9 152.3 %all-reduce.4.cloned.1.call-start = ((), (), s32[]{:S(2)}) async-start(), calls=%async_computation.2 | async-start | bytes 4194304 | tf_op jit(solution)/shard_map/psum | solution.py:22
  32.3 152.1 %all-reduce.6.cloned.1.call-start = ((), (), s32[]{:S(2)}) async-start(), calls=%async_computation.3 | async-start | bytes 524288 | tf_op jit(solution)/shard_map/psum | solution.py:26
  160.2 86.0 %copy-start.2 = (f32[2048,256]{1,0:T(8,128)S(1)}, f32[2048,256]{1,0:T(8,128)}, u32[]{:S(2)}) copy-start(f32[2048,256]{1,0:T(8,128)} %all-reduce.4.cloned.1.call-done) | copy-start | bytes 6291460
  166.8 109.9 %reduce-scatter.2.cloned.1.call-start = ((), (), s32[]{:S(2)}) async-start(), calls=%async_computation.4 | async-start | bytes 1572864 | tf_op jit(solution)/shard_map/reduce_scatter | solution.py:32
  246.2 4.0 %copy-start = (bf16[2048,1024]{1,0:T(8,128)(2,1)S(1)}, bf16[2048,1024]{1,0:T(8,128)(2,1)}, u32[]{:S(2)}) copy-start(bf16[2048,1024]{1,0:T(8,128)(2,1)} %param.3) | copy-start | bytes 12582916
  266.9 53.6 %all-gather.5.cloned.1.call-start = ((), (), s32[]{:S(2)}) async-start(), calls=%async_computation.5 | async-start | bytes 1572864 | tf_op jit(solution)/shard_map/all_gather | solution.py:36
  320.5 16.1 %copy-start.1 = (bf16[2048,1024]{1,0:T(8,128)(2,1)S(1)}, bf16[2048,1024]{1,0:T(8,128)(2,1)}, u32[]{:S(2)}) copy-start(bf16[2048,1024]{1,0:T(8,128)(2,1)} %param.3) | copy-start | bytes 12582916
  320.5 16.1 %copy-start.3 = (f32[1024,256]{1,0:T(8,128)S(1)}, f32[1024,256]{1,0:T(8,128)}, u32[]{:S(2)}) copy-start(f32[1024,256]{1,0:T(8,128)} %all-gather.5.cloned.1.call-done) | copy-start | bytes 3145732
Sparse Core Ops, SparseCore 0:
  9.5 11.7 all-gather.2
  32.4 127.7 all-reduce.3
  166.9 17.4 all-reduce.5
  267.0 9.5 reduce-scatter.1
  278.0 10.2 all-gather.4
where the time goes:
time: 368 us; the launch traced here: 362 us
  waiting for transfers between devices  169 us (46%)
  matrix products  73.1 us (20%)
  other arithmetic  57.7 us (16%)
  blocking collectives  40.8 us (11%)
  between operations  15.5 us (4%)
  local copies, waits for them, and re-layouts  5.14 us (1%)
    psum x1, waiting for transfers between devices, body(): left = lax.psum(partial_value, 'col')  128 us
    psum x1, blocking collectives, body(): squares_right = lax.psum(jnp.sum(share * share, axis=0), ('col', 'row'))  40.8 us
    another operation x6, other arithmetic, body(): lower = jnp.linalg.cholesky(gram)  34 us
    another operation x3, other arithmetic, body(): left_orth = jax.scipy.linalg.solve_triangular(lower, left.T, lower=True).T  19.7 us
    dot_general x1, matrix products, body(): lax.dot_general(left_orth, right_whole, contract_cols, precision=highest,...  18.4 us
    psum x1, waiting for transfers between devices, body(): gram = lax.psum(local_gram, 'row')  17 us
    dot_general x1, matrix products, body(): lax.dot_general(blend, left_orth, contract_rows, precision=highest, prefe...  16.6 us
    dot_general x1, matrix products, body(): lax.dot_general(left_orth, right_unit, contract_cols, precision=highest,...  16.1 us
  transfers between devices with their start and end apart: 5, of which 4 were waited for; matrix products, arithmetic and copies ran while one was open for 1% of the time, Pallas kernels for 0%

commit v1 on v0

--- a/solution.py
+++ b/solution.py
@@ -19,7 +19,9 @@
     partial_value = jnp.dot(
         blend, right_block, precision=highest, preferred_element_type=jnp.float32
     )
-    left = lax.psum(partial_value, "col")
+    left = partial_value
+    for hop in (1, 2, 4, 8):
+        left = left + lax.ppermute(left, "col", [(dev, dev ^ hop) for dev in range(16)])
     local_gram = lax.dot_general(
         left, left, contract_rows, precision=highest, preferred_element_type=jnp.float32
     )

time: 368 us -> 475 us (1.29)
  waiting for transfers between devices: 169 us -> 264 us
  starting transfers between devices: 0.73 us -> 8.83 us
    ppermute x0 -> x4, waiting for transfers between devices: none -> 224 us  [body(): lax.ppermute(left, 'col', [(dev, dev ^ hop) for dev in range(16)])]
    psum x1 -> x0, waiting for transfers between devices: 128 us -> none  [body(): left = lax.psum(partial_value, 'col')]
    ppermute x0 -> x4, starting transfers between devices: none -> 8.14 us  [body(): lax.ppermute(left, 'col', [(dev, dev ^ hop) for dev in range(16)])]
  transfers between devices with their start and end apart: 5 -> 8, of which waited for: 4 -> 7; matrix products, arithmetic and copies ran while one was open for 1% -> 1% of each run, Pallas kernels for 0% -> 0%
where the time goes in v1:
time: 475 us; the launch traced here: 468 us
  waiting for transfers between devices  264 us (56%)
  matrix products  72 us (15%)
  other arithmetic  61.7 us (13%)
  blocking collectives  40.8 us (9%)
  between operations  15.7 us (3%)
  starting transfers between devices  8.83 us (2%)
  local copies, waits for them, and re-layouts  5.07 us (1%)
    ppermute x4, waiting for transfers between devices, body(): lax.ppermute(left, 'col', [(dev, dev ^ hop) for dev in range(16)])  224 us
    psum x1, blocking collectives, body(): squares_right = lax.psum(jnp.sum(share * share, axis=0), ('col', 'row'))  40.8 us
    another operation x6, other arithmetic, body(): lower = jnp.linalg.cholesky(gram)  34 us
    another operation x3, other arithmetic, body(): left_orth = jax.scipy.linalg.solve_triangular(lower, left.T, lower=True).T  19.7 us
    dot_general x1, matrix products, body(): lax.dot_general(left_orth, right_whole, contract_cols, precision=highest,...  18.4 us
    dot_general x1, matrix products, body(): lax.dot_general(blend, left_orth, contract_rows, precision=highest, prefe...  16.6 us
    dot_general x1, matrix products, body(): lax.dot_general(left_orth, right_unit, contract_cols, precision=highest,...  16.1 us
    psum x1, waiting for transfers between devices, body(): gram = lax.psum(local_gram, 'row')  15.8 us
  transfers between devices with their start and end apart: 8, of which 7 were waited for; matrix products, arithmetic and copies ran while one was open for 1% of the time, Pallas kernels for 0%

profile of v1, /device:TPU:0, one launch (start us, length us, event | category | flops | bytes accessed | tf_op | source)
XLA Modules:
  0.0 468.1 jit_solution(8619989926110456937)
XLA Ops:
  7.2 0.0 all-gather.3.cloned.1.call-start
  7.2 0.7 all-gather.3.cloned.1.call-update
  7.9 0.0 all-reduce.3.cloned.1.call-start
  7.9 13.4 %all-gather.3.cloned.1.call-done = f32[1024,256]{1,0:T(8,128)} async-done(((f32[512,256]{1,0:T(8,128)}), f32[1024,256]{1,0:T(8,128)}) %all-gather.3.cloned.1.call-update) | async-done | bytes 1048592 | tf_op jit(solution)/shard_map/all_gather | solution.py:17
  21.3 10.0 %fusion.1 = f32[2048,256]{1,0:T(8,128)S(1)} fusion(f32[1024,256]{1,0:T(8,128)} %all-gather.3.cloned.1.call-done, f32[2048,1024]{1,0:T(8,128)} %param.4, bf16[2048,1024]{1,0:T(8,128)(2,1)} %param.3), kind=kOutput, calls=%fused_computation.6 | convolution fusion | flops 6446645248 | bytes 15728640 | tf_op jit(solution)/shard_map/dot_general | solution.py:19
  31.3 1.8 collective-permute-start
  33.1 46.1 %collective-permute-done = f32[2048,256]{1,0:T(8,128)S(1)} collective-permute-done((f32[2048,256]{1,0:T(8,128)S(1)}, f32[2048,256]{1,0:T(8,128)S(1)}, u32[]{:S(2)}, u32[]{:S(2)}) %collective-permute-start) | collective-permute-done | bytes 2097184 | tf_op jit(solution)/shard_map/ppermute | solution.py:24
  79.2 0.3 add.51
  79.5 1.8 collective-permute-start.1
  81.3 45.2 %collective-permute-done.1 = f32[2048,256]{1,0:T(8,128)S(1)} collective-permute-done((f32[2048,256]{1,0:T(8,128)S(1)}, f32[2048,256]{1,0:T(8,128)S(1)}, u32[]{:S(2)}, u32[]{:S(2)}) %collective-permute-start.1) | collective-permute-done | bytes 2097184 | tf_op jit(solution)/shard_map/ppermute | solution.py:24
  126.5 0.3 add.52
  126.8 1.8 collective-permute-start.2
  128.6 44.4 %collective-permute-done.2 = f32[2048,256]{1,0:T(8,128)S(1)} collective-permute-done((f32[2048,256]{1,0:T(8,128)S(1)}, f32[2048,256]{1,0:T(8,128)S(1)}, u32[]{:S(2)}, u32[]{:S(2)}) %collective-permute-start.2) | collective-permute-done | bytes 2097184 | tf_op jit(solution)/shard_map/ppermute | solution.py:24
  173.0 0.3 add.53
  173.3 2.7 collective-permute-start.3
  176.0 88.6 %collective-permute-done.3 = f32[2048,256]{1,0:T(8,128)} collective-permute-done((f32[2048,256]{1,0:T(8,128)S(1)}, f32[2048,256]{1,0:T(8,128)}, u32[]{:S(2)}, u32[]{:S(2)}) %collective-permute-start.3) | collective-permute-done | bytes 2097184 | tf_op jit(solution)/shard_map/ppermute | solution.py:24
  264.5 6.4 %fusion.6 = f32[256,256]{0,1:T(8,128)} fusion(f32[2048,256]{1,0:T(8,128)S(1)} %add.53, f32[2048,256]{1,0:T(8,128)} %collective-permute-done.3), kind=kOutput, calls=%fused_computation.15 | convolution fusion | flops 1611137024 | bytes 4456448 | tf_op jit(solution)/shard_map/dot_general | solution.py:25
  271.0 0.0 all-reduce.3.cloned.1.call-update
  271.0 0.6 reduce-scatter.2.cloned.1.call-start
  271.6 3.2 add_bitcast_fusion
  274.7 0.0 copy-start.2
  274.7 15.8 %all-reduce.3.cloned.1.call-done = f32[256,256]{0,1:T(8,128)} async-done(((f32[256,256]{0,1:T(8,128)}), f32[256,256]{0,1:T(8,128)}) %all-reduce.3.cloned.1.call-update) | async-done | bytes 262160 | tf_op jit(solution)/shard_map/psum | solution.py:28
  290.5 1.1 copy.7
  291.6 1.0 fusion.9
  292.6 11.7 %cholesky.50 = f32[128,128]{1,0:T(8,128)S(1)} custom-call(f32[128,128]{1,0:T(8,128)S(1)} %cholesky.118), custom_call_target="Cholesky" | custom-call | tf_op jit(solution)/shard_map/jit(cholesky)/cholesky | solution.py:29
  304.3 9.8 %custom-call.15 = f32[1,128,128]{1,2,0:T(8,128)S(1)} custom-call(f32[1,128,128]{2,1,0:T(8,128)S(1)} %get-tuple-element.24), custom_call_target="InvertDiagBlocksLowerTriangular" | custom-call | tf_op jit(solution)/shard_map/jit(cholesky)/cholesky | solution.py:29
  314.2 0.2 constant_dynamic-update-slice_fusion.1
  314.4 0.3 convolution_subtract_fusion
  314.7 11.7 %cholesky.105 = f32[128,128]{1,0:T(8,128)S(1)} custom-call(f32[128,128]{1,0:T(8,128)S(1)} %convolution_subtract_fusion), custom_call_target="Cholesky" | custom-call | tf_op jit(solution)/shard_map/jit(cholesky)/cholesky | solution.py:29
  326.4 0.7 compare_reduce_fusion
  328.4 0.1 triangular_solve.57
  328.5 4.1 while.1
  328.6 0.6 fusion.25
  329.2 1.3 bitcast_dynamic-update-slice_fusion.2
  330.6 0.6 fusion.25
  331.2 1.3 bitcast_dynamic-update-slice_fusion.2
  332.5 19.7 %custom-call.16 = f32[2,128,128]{1,2,0:T(8,128)S(1)} custom-call(f32[2,128,128]{2,1,0:T(8,128)S(1)} %get-tuple-element.10), custom_call_target="InvertDiagBlocksLowerTriangular" | custom-call | tf_op jit(solution)/shard_map/jit(_solve_triangular)/triangular_solve | solution.py:30
  352.2 0.0 copy-done.2
  352.2 0.0 copy-start.3
  352.3 1.1 fusion.3
  353.3 0.0 copy-start
  353.3 1.8 fusion.10
  355.2 0.0 copy-done.3
  355.2 1.1 fusion.2
  356.2 0.0 copy-done
  356.3 16.6 %fusion = f32[1024,256]{1,0:T(8,128)} fusion(f32[2048,1024]{1,0:T(8,128)} %param.4, bf16[2048,1024]{1,0:T(8,128)(2,1)S(1)} %copy-done, f32[128,2048]{1,0:T(8,128)S(1)} %fusion.2, f32[128,2048]{1,0:T(8,128)S(1)} %fusion.3), kind=kOutput, calls=%fused_computation.5 | convolution fusion | flops 6447169536 | bytes 15728640 | tf_op jit(solution)/shard_map/dot_general | solution.py:31
  372.9 0.0 reduce-scatter.2.cloned.1.call-update
  372.9 0.0 all-gather.5.cloned.1.call-start
  373.0 9.7 %reduce-scatter.2.cloned.1.call-done = f32[512,256]{1,0:T(8,128)} async-done(((f32[1024,256]{1,0:T(8,128)}), f32[512,256]{1,0:T(8,128)}) %reduce-scatter.2.cloned.1.call-update) | async-done | bytes 524304 | tf_op jit(solution)/shard_map/reduce_scatter | solution.py:34
  382.7 0.0 all-gather.5.cloned.1.call-update
  382.7 1.1 multiply_reduce_fusion
  383.8 40.8 %psum.15 = f32[256]{0:T(256)S(1)} all-reduce(f32[256]{0:T(256)S(1)} %multiply_reduce_fusion), channel_id=1, replica_groups=mesh['col'=16,'row'=2] {'col','row'}, use_global_device_ids=true, to_apply=%region_7.8 | all-reduce | flops 256 | bytes 2048 | tf_op jit(solution)/shard_map/psum | solution.py:35
  424.6 1.9 broadcast_divide_fusion
  426.5 0.0 all-gather.5.cloned.1.call-done
  426.5 0.0 copy-start.1
  426.5 0.0 copy-start.4
  426.5 16.1 %multiply_convert_fusion = bf16[2048,1024]{1,0:T(8,128)(2,1)} fusion(f32[128,2048]{1,0:T(8,128)S(1)} %fusion.2, f32[128,2048]{1,0:T(8,128)S(1)} %fusion.3, f32[1024,256]{1,0:T(8,128)} %all-gather.5.cloned.1.call-done, f32[256]{0:T(256)S(1)} %add_sqrt_fusion), kind=kOutput, calls=%fused_computation.2 | convolution fusion | flops 6447431680 | bytes 7341056 | tf_op jit(solution)/shard_map/dot_general | solution.py:46
  442.6 0.0 copy-done.1
  442.6 0.0 copy-done.4
  442.6 18.4 %multiply_subtract_fusion = f32[2048,1024]{1,0:T(8,128)} fusion(f32[1024,256]{1,0:T(8,128)S(1)} %copy-done.4, f32[2048,1024]{1,0:T(8,128)} %param.4, bf16[2048,1024]{1,0:T(8,128)(2,1)S(1)} %copy-done.1, f32[128,2048]{1,0:T(8,128)S(1)} %fusion.2, f32[128,2048]{1,0:T(8,128)S(1)} %fusion.3), kind=kOutput, calls=%fused_computation.3 | convolution fusion | flops 6451363840 | bytes 24117248 | tf_op jit(solution)/shard_map/dot_general | solution.py:41
  (10 shorter events, 0.2 us)
Async XLA Ops:
  7.2 14.1 %all-gather.3.cloned.1.call-start = ((), (), s32[]{:S(2)}) async-start(), calls=%async_computation.1 | async-start | bytes 1572864 | tf_op jit(solution)/shard_map/all_gather | solution.py:17
  7.9 282.6 %all-reduce.3.cloned.1.call-start = ((), (), s32[]{:S(2)}) async-start(), calls=%async_computation.2 | async-start | bytes 524288 | tf_op jit(solution)/shard_map/psum | solution.py:28
  31.3 47.9 %collective-permute-start = (f32[2048,256]{1,0:T(8,128)S(1)}, f32[2048,256]{1,0:T(8,128)S(1)}, u32[]{:S(2)}, u32[]{:S(2)}) collective-permute-start(f32[2048,256]{1,0:T(8,128)S(1)} %fusion.1), channel_id=1, source_target_pairs={{0,2},{2,0},{4,6},{6,4},{8,10},{10,8},{12,14},{14,12},{16,18},{18,... | collective-permute-start | bytes 6291464 | tf_op jit(solution)/shard_map/ppermute | solution.py:24
  79.5 47.0 %collective-permute-start.1 = (f32[2048,256]{1,0:T(8,128)S(1)}, f32[2048,256]{1,0:T(8,128)S(1)}, u32[]{:S(2)}, u32[]{:S(2)}) collective-permute-start(f32[2048,256]{1,0:T(8,128)S(1)} %add.51), channel_id=1, source_target_pairs={{0,4},{2,6},{4,0},{6,2},{8,12},{10,14},{12,8},{14,10},{16,20},{18,... | collective-permute-start | bytes 6291464 | tf_op jit(solution)/shard_map/ppermute | solution.py:24
  126.8 46.2 %collective-permute-start.2 = (f32[2048,256]{1,0:T(8,128)S(1)}, f32[2048,256]{1,0:T(8,128)S(1)}, u32[]{:S(2)}, u32[]{:S(2)}) collective-permute-start(f32[2048,256]{1,0:T(8,128)S(1)} %add.52), channel_id=1, source_target_pairs={{0,8},{2,10},{4,12},{6,14},{8,0},{10,2},{12,4},{14,6},{16,24},{18,... | collective-permute-start | bytes 6291464 | tf_op jit(solution)/shard_map/ppermute | solution.py:24
  173.3 91.3 %collective-permute-start.3 = (f32[2048,256]{1,0:T(8,128)S(1)}, f32[2048,256]{1,0:T(8,128)}, u32[]{:S(2)}, u32[]{:S(2)}) collective-permute-start(f32[2048,256]{1,0:T(8,128)S(1)} %add.53), channel_id=1, source_target_pairs={{0,16},{2,18},{4,20},{6,22},{8,24},{10,26},{12,28},{14,30},{16,0},... | collective-permute-start | bytes 6291464 | tf_op jit(solution)/shard_map/ppermute | solution.py:24
  271.0 111.7 %reduce-scatter.2.cloned.1.call-start = ((), (), s32[]{:S(2)}) async-start(), calls=%async_computation.3 | async-start | bytes 1572864 | tf_op jit(solution)/shard_map/reduce_scatter | solution.py:34
  274.7 77.5 %copy-start.2 = (f32[256,2048]{0,1:T(8,128)S(1)}, f32[256,2048]{0,1:T(8,128)}, u32[]{:S(2)}) copy-start(f32[256,2048]{0,1:T(8,128)} %add_bitcast_fusion) | copy-start | bytes 6291460
  352.2 2.9 copy-start.3
  353.3 2.9 copy-start
  372.9 53.6 %all-gather.5.cloned.1.call-start = ((), (), s32[]{:S(2)}) async-start(), calls=%async_computation.4 | async-start | bytes 1572864 | tf_op jit(solution)/shard_map/all_gather | solution.py:38
  426.5 16.1 %copy-start.1 = (bf16[2048,1024]{1,0:T(8,128)(2,1)S(1)}, bf16[2048,1024]{1,0:T(8,128)(2,1)}, u32[]{:S(2)}) copy-start(bf16[2048,1024]{1,0:T(8,128)(2,1)} %param.3) | copy-start | bytes 12582916
  426.5 16.1 %copy-start.4 = (f32[1024,256]{1,0:T(8,128)S(1)}, f32[1024,256]{1,0:T(8,128)}, u32[]{:S(2)}) copy-start(f32[1024,256]{1,0:T(8,128)} %all-gather.5.cloned.1.call-done) | copy-start | bytes 3145732
Sparse Core Ops, SparseCore 0:
  9.5 11.7 all-gather.2
  271.1 19.3 all-reduce.2
  373.0 9.5 reduce-scatter.1
  384.1 10.2 all-gather.4
